TPU v7x, 32 devices: a whole 2x2x4 slice. The times are simulated.
32 devices in a mesh: gy: 8 (over z, y), gz: 4 (over x, core).
Axes of the slice: x: 2, y: 2, z: 4, core: 2. Of those that a mesh axis runs over, the one named last changes fastest.
Arguments:
- tokens: bfloat16 [2, 64, 8, 8, 1024], P(None, None, 'gy', 'gz'), may hold values from -64 to 64
- w_qkv: bfloat16 [1024, 3072], P('gy'), may hold values from -2 to 2
- w_out: bfloat16 [1024, 1024], P('gy'), may hold values from -0.1875 to 0.1875
- bias_x: float32 [16, 127], replicated, may hold values from -4 to 4
- bias_y: float32 [16, 15], replicated, may hold values from -4 to 4
- bias_z: float32 [16, 15], replicated, may hold values from -4 to 4
Outputs:
- mixed: bfloat16 [2, 64, 8, 8, 1024], P(None, None, 'gy', 'gz')
All inputs are finite; a program needn't handle non-finite values.
Results may differ from a plain program's by a relative error of at most 0.0083.
Values may be sent and summed in bfloat16 or wider, within the bound.
A program may use at most 64 MiB of HBM per device.

v0:
```python
import jax
import jax.numpy as jnp
from jax import lax
from jax.sharding import PartitionSpec as P

HEADS = 16
HEAD = 64


einsum_forms = {
    1: ("bxyzhs,bwyzhs->byzhxw", "byzhxw,bwyzhs->bxyzhs"),
    2: ("bxyzhs,bxwzhs->bxzhyw", "bxzhyw,bxwzhs->bxyzhs"),
    3: ("bxyzhs,bxywhs->bxyhzw", "bxyhzw,bxywhs->bxyzhs"),
}


def norm_rows(tokens):
    values = tokens.astype(jnp.float32)
    center = jnp.mean(values, axis=-1, keepdims=True)
    spread = jnp.mean((values - center) ** 2, axis=-1, keepdims=True)
    return ((values - center) * lax.rsqrt(spread + 1e-05)).astype(jnp.bfloat16)


def rel_bias(table):
    length = (table.shape[1] + 1) // 2
    offsets = (
        lax.broadcasted_iota(jnp.int32, (length, length), 0)
        - lax.broadcasted_iota(jnp.int32, (length, length), 1)
        + length
        - 1
    )
    lookup = (
        offsets[:, :, None] == lax.broadcasted_iota(jnp.int32, (1, 1, 2 * length - 1), 2)
    ).astype(jnp.float32)
    return jnp.einsum("hr,ijr->hij", table, lookup, precision=lax.Precision.HIGHEST)


def attend(qkv, table, axis):
    dims = qkv.shape
    features = dims[-1] // 3
    parts = qkv.reshape(dims[:-1] + (3, HEADS, HEAD))
    query = parts[..., 0, :, :]
    keys = parts[..., 1, :, :]
    values = parts[..., 2, :, :]
    score_form, mix_form = einsum_forms[axis]
    scores = jnp.einsum(score_form, query, keys, preferred_element_type=jnp.float32) * HEAD ** (
        -0.5
    ) + rel_bias(table)
    scores = scores - jnp.max(scores, axis=-1, keepdims=True)
    expo = jnp.exp(scores)
    weights = (expo / jnp.sum(expo, axis=-1, keepdims=True)).astype(jnp.bfloat16)
    mixed = jnp.einsum(mix_form, weights, values, preferred_element_type=jnp.float32)
    return mixed.reshape(dims[:-1] + (features,)).astype(jnp.bfloat16)


def return_y(result):
    return lax.all_to_all(result, "gy", split_axis=2, concat_axis=1, tiled=True)


def return_z(result):
    return lax.all_to_all(result, "gz", split_axis=3, concat_axis=1, tiled=True)


def shards(tokens, w_qkv, w_out, bias_x, bias_y, bias_z):
    samples, depth, rows_y, rows_z, features = tokens.shape
    normed = norm_rows(tokens)
    gathered = lax.all_gather(w_qkv, "gy", axis=0, tiled=True)

    def project(inputs):
        product = jnp.dot(
            inputs.reshape(-1, features), gathered, preferred_element_type=jnp.float32
        )
        return product.astype(jnp.bfloat16).reshape(inputs.shape[:-1] + (3 * features,))

    along_x = attend(project(normed), bias_x, 1)
    along_y = return_y(
        attend(
            project(lax.all_to_all(normed, "gy", split_axis=1, concat_axis=2, tiled=True)),
            bias_y,
            2,
        )
    )
    along_z = return_z(
        attend(
            project(lax.all_to_all(normed, "gz", split_axis=1, concat_axis=3, tiled=True)),
            bias_z,
            3,
        )
    )
    summed = along_x.astype(jnp.float32) + along_y.astype(jnp.float32) + along_z.astype(jnp.float32)
    summed = summed.astype(jnp.bfloat16).reshape(-1, features)
    residual = tokens.reshape(-1, features).astype(jnp.float32)
    result = residual + jnp.dot(
        summed, lax.all_gather(w_out, "gy", axis=0, tiled=True), preferred_element_type=jnp.float32
    )
    return result.astype(jnp.bfloat16).reshape(tokens.shape)


def solution(mesh):
    placed = (P(None, None, "gy", "gz", None), P("gy", None), P("gy", None), P(), P(), P())
    return jax.shard_map(
        shards,
        mesh=mesh,
        in_specs=placed,
        out_specs=P(None, None, "gy", "gz", None),
        check_vma=False,
    )
```

profile of v0, /device:TPU:0, one launch (start us, length us, event | category | flops | bytes accessed | tf_op | source)
XLA Modules:
  0.0 212.9 jit_solution(13488122357055576503)
XLA Ops:
  12.3 4.2 %all-to-all-start.2 = ((bf16[2,64,1,2,1024]{4,3,2,0,1:T(2,128)(2,1)}), bf16[2,64,1,2,1024]{4,3,2,0,1:T(2,128)(2,1)S(1)}, u32[]{:S(2)}, u32[]{:S(2)}) async-start(bf16[2,64,1,2,1024]{4,3,2,0,1:T(2,128)(2,1)} %multiply_convert_fusion), calls=%async_computation.2 | async-start | bytes 1048576 | tf_op jit(solution)/shard_map/all_to_all | solution.py:85
  17.3 8.1 %all-to-all-done.2 = bf16[2,64,1,2,1024]{4,3,2,0,1:T(2,128)(2,1)S(1)} async-done(((bf16[2,64,1,2,1024]{4,3,2,0,1:T(2,128)(2,1)}), bf16[2,64,1,2,1024]{4,3,2,0,1:T(2,128)(2,1)S(1)}, u32[]{:S(2)}, u32[]{:S(2)}) %all-to-all-start.2) | async-done | bytes 524320 | tf_op jit(solution)/shard_map/all_to_all | solution.py:85
  25.4 6.5 %all-to-all-start = ((bf16[2,64,1,2,1024]{4,3,2,0,1:T(2,128)(2,1)}), bf16[2,64,1,2,1024]{4,3,2,0,1:T(2,128)(2,1)S(1)}, u32[]{:S(2)}, u32[]{:S(2)}) async-start(bf16[2,64,1,2,1024]{4,3,2,0,1:T(2,128)(2,1)} %multiply_convert_fusion), calls=%async_computation | async-start | bytes 1048576 | tf_op jit(solution)/shard_map/all_to_all | solution.py:78
  35.0 3.2 %fusion.11 = f32[16,64,64]{2,0,1:T(8,128)S(1)} fusion(s32[64,64]{1,0:T(8,128)S(1)} %subtract_add_fusion, f32[16,127]{1,0:T(8,128)S(1)} %copy-done), kind=kOutput, calls=%fused_computation.29 | convolution fusion | flops 100397056 | bytes 286656 | tf_op jit(solution)/shard_map/hr,ijr->hij/dot_general | solution.py:35
  42.4 17.7 %all-to-all-done = bf16[2,64,1,2,1024]{4,3,2,0,1:T(2,128)(2,1)S(1)} async-done(((bf16[2,64,1,2,1024]{4,3,2,0,1:T(2,128)(2,1)}), bf16[2,64,1,2,1024]{4,3,2,0,1:T(2,128)(2,1)S(1)}, u32[]{:S(2)}, u32[]{:S(2)}) %all-to-all-start) | async-done | bytes 524320 | tf_op jit(solution)/shard_map/all_to_all | solution.py:78
  61.5 60.6 %all-gather.3.cloned.1.call-done = bf16[1024,3072]{1,0:T(8,128)(2,1)} async-done(((bf16[128,3072]{1,0:T(8,128)(2,1)}), bf16[1024,3072]{1,0:T(8,128)(2,1)}) %all-gather.3.cloned.1.call-update) | async-done | bytes 6291472 | tf_op jit(solution)/shard_map/all_gather | solution.py:67
  122.1 5.8 %convolution_convert_fusion = bf16[256,3072]{1,0:T(8,128)(2,1)} fusion(bf16[256,1024]{1,0:T(8,128)(2,1)S(1)} %reshape.182, bf16[1024,3072]{1,0:T(8,128)(2,1)} %all-gather.3.cloned.1.call-done), kind=kOutput, calls=%fused_computation.3 | convolution fusion | flops 1611399168 | bytes 8388608 | tf_op jit(solution)/shard_map/dot_general | solution.py:70
  127.9 3.6 %reshape_reshape.11 = bf16[2,16,1,8,3,16,64]{6,5,4,3,1,0,2:T(8,128)(2,1)S(1)} reshape(bf16[256,3072]{1,0:T(8,128)(2,1)} %convolution_convert_fusion) | data formatting | bytes 3145728 | tf_op jit(solution)/shard_map/reshape;reshape | solution.py:41
  133.7 5.9 %convolution_convert_fusion.1 = bf16[256,3072]{1,0:T(8,128)(2,1)} fusion(bf16[256,1024]{1,0:T(8,128)(2,1)S(1)} %copy-done.10, bf16[1024,3072]{1,0:T(8,128)(2,1)} %all-gather.3.cloned.1.call-done), kind=kOutput, calls=%fused_computation.4 | convolution fusion | flops 1611399168 | bytes 8388608 | tf_op jit(solution)/shard_map/dot_general | solution.py:70
  139.6 3.0 %fusion.37 = (f32[2,16,16,8]{3,2,1,0:T(8,128)S(1)}, f32[2,16,16,8,8]{3,4,2,1,0:T(8,128)}) fusion(f32[16,8,8]{1,2,0:T(8,128)S(1)} %copy.97, bf16[2,16,1,8,1,16,64]{6,5,4,3,1,0,2:T(8,128)(2,1)S(1)} %copy-done.8, bf16[2,16,1,8,1,16,64]{6,5,4,3,1,0,2:T(8,128)(2,1)S(1)} %copy-done.7), kind=kOutput, calls=%fused_computation.79 | convolution fusion | flops 4325383 | bytes 1200128 | tf_op jit(solution)/shard_map/sub | solution.py:49
  142.7 3.6 %reshape_reshape.10 = bf16[2,8,8,2,3,16,64]{6,5,4,3,2,1,0:T(8,128)(2,1)S(1)} reshape(bf16[256,3072]{1,0:T(8,128)(2,1)} %convolution_convert_fusion.1) | data formatting | bytes 3145728 | tf_op jit(solution)/shard_map/reshape;reshape | solution.py:41
  146.3 2.7 %fusion.9 = bf16[2,16,1,8,16,64]{5,3,4,1,0,2:T(8,128)(2,1)S(1)} fusion(f32[2,16,16,8,8]{3,4,2,1,0:T(8,128)} %get-tuple-element.15, bf16[2,16,1,8,1,16,64]{6,5,4,3,1,0,2:T(8,128)(2,1)} %get-tuple-element.11, f32[2,16,16,8]{3,2,1,0:T(8,128)S(1)} %get-tuple-element.14), kind=kOutput, calls=%fused_computation.26 | convolution fusion | flops 4521984 | bytes 1196032 | tf_op jit(solution)/shard_map/bxyhzw,bxywhs->bxyzhs/dot_general | solution.py:52
  150.4 2.6 %reshape.198 = bf16[2,16,1,8,1024]{4,1,0,2,3:T(8,128)(2,1)} reshape(bf16[2,16,1,8,16,64]{5,4,1,0,3,2:T(8,128)(2,1)} %copy.108) | data formatting | bytes 1048576 | tf_op jit(solution)/shard_map/convert_element_type | solution.py:53
  153.0 4.4 %all-to-all-start.3 = ((bf16[2,16,1,8,1024]{4,1,0,2,3:T(8,128)(2,1)}), bf16[2,16,1,8,1024]{4,1,0,2,3:T(8,128)(2,1)}, u32[]{:S(2)}, u32[]{:S(2)}) async-start(bf16[2,16,1,8,1024]{4,1,0,2,3:T(8,128)(2,1)} %reshape.198), calls=%async_computation.3 | async-start | bytes 1048576 | tf_op jit(solution)/shard_map/all_to_all | solution.py:61
  157.3 2.2 %fusion.34 = (bf16[2,8,8,2,1,16,64]{6,5,4,3,2,1,0:T(8,128)(2,1)}, bf16[2,8,8,2,1,16,64]{6,5,4,3,2,1,0:T(8,128)(2,1)}, bf16[2,8,8,2,1,16,64]{6,5,4,3,2,1,0:T(8,128)(2,1)}) fusion(bf16[2,8,8,2,3,16,64]{6,5,4,3,2,1,0:T(8,128)(2,1)S(1)} %reshape_reshape.10), kind=kLoop, calls=%fused_computation.76 | loop fusion | bytes 3145728 | tf_op jit(solution)/shard_map/slice | solution.py:44
  159.6 3.4 %fusion.39 = (f32[2,8,2,16,8]{4,3,2,1,0:T(8,128)S(1)}, f32[2,8,2,16,8,8]{4,5,3,2,1,0:T(8,128)S(1)}) fusion(f32[16,8,8]{1,2,0:T(8,128)S(1)} %copy.88, bf16[2,8,8,2,1,16,64]{6,5,4,3,2,1,0:T(8,128)(2,1)} %get-tuple-element.7, bf16[2,8,8,2,1,16,64]{6,5,4,3,2,1,0:T(8,128)(2,1)} %get-tuple-element.6), kind=kOutput, calls=%fused_computation.81 | convolution fusion | flops 4325383 | bytes 1200128 | tf_op jit(solution)/shard_map/sub | solution.py:49
  163.0 6.0 %convolution_convert_fusion.2 = bf16[256,3072]{1,0:T(8,128)(2,1)} fusion(bf16[256,1024]{1,0:T(8,128)(2,1)S(1)} %copy-done.9, bf16[1024,3072]{1,0:T(8,128)(2,1)} %all-gather.3.cloned.1.call-done), kind=kOutput, calls=%fused_computation.5 | convolution fusion | flops 1611399168 | bytes 8388608 | tf_op jit(solution)/shard_map/dot_general | solution.py:70
  171.5 3.6 %reshape_reshape.9 = bf16[2,64,1,2,3,16,64]{6,5,4,3,1,0,2:T(8,128)(2,1)S(1)} reshape(bf16[256,3072]{1,0:T(8,128)(2,1)} %convolution_convert_fusion.2) | data formatting | bytes 3145728 | tf_op jit(solution)/shard_map/reshape;reshape | solution.py:41
  177.0 2.3 %copy.111 = bf16[2,64,1,2,1,16,64]{1,6,5,3,0,4,2:T(8,128)(2,1)S(1)} copy(bf16[2,64,1,2,1,16,64]{6,5,4,3,1,0,2:T(8,128)(2,1)} %get-tuple-element.8) | data formatting | bytes 1048576
  179.4 4.4 %all-to-all-start.1 = ((bf16[2,8,8,2,1024]{4,3,1,0,2:T(2,128)(2,1)}), bf16[2,8,8,2,1024]{4,3,1,0,2:T(2,128)(2,1)}, u32[]{:S(2)}, u32[]{:S(2)}) async-start(bf16[2,8,8,2,1024]{4,3,1,0,2:T(2,128)(2,1)} %reshape.197), calls=%async_computation.1 | async-start | bytes 1048576 | tf_op jit(solution)/shard_map/all_to_all | solution.py:57
  183.8 3.7 %fusion.38 = (f32[2,2,16,64]{3,2,1,0:T(8,128)S(1)}, f32[2,2,16,64,64]{3,4,2,1,0:T(8,128)}) fusion(f32[16,64,64]{1,2,0:T(8,128)} %copy.81, bf16[2,64,1,2,1,16,64]{6,5,4,3,1,0,2:T(8,128)(2,1)S(1)} %copy-done.4, bf16[2,64,1,2,1,16,64]{6,5,4,3,1,0,2:T(8,128)(2,1)S(1)} %copy-done.5), kind=kOutput, calls=%fused_computation.80 | convolution fusion | flops 34603072 | bytes 2375680 | tf_op jit(solution)/shard_map/sub | solution.py:49
  187.5 3.4 %convert_bitcast_fusion = f32[2,64,1,2,16,64]{1,5,4,3,0,2:T(8,128)} fusion(f32[2,2,16,64,64]{3,4,2,1,0:T(8,128)} %get-tuple-element.17, bf16[2,64,1,2,1,16,64]{1,6,5,3,0,4,2:T(8,128)(2,1)S(1)} %copy.111, f32[2,2,16,64]{3,2,1,0:T(8,128)S(1)} %get-tuple-element.16), kind=kOutput, calls=%fused_computation.6 | convolution fusion | flops 34603008 | bytes 2637824 | tf_op jit(solution)/shard_map/byzhxw,bwyzhs->bxyzhs/dot_general | solution.py:52
  190.9 3.1 %copy.83 = f32[2,64,1,2,16,64]{5,4,3,1,0,2:T(8,128)S(1)} copy(f32[2,64,1,2,16,64]{1,5,4,3,0,2:T(8,128)} %convert_bitcast_fusion) | data formatting | bytes 2097152 | tf_op jit(solution)/shard_map/convert_element_type | solution.py:90
  201.9 3.1 %fusion.10 = bf16[256,1024]{1,0:T(8,128)(2,1)S(1)} fusion(f32[256,1024]{1,0:T(8,128)S(1)} %copy-done.3, bf16[1024,1024]{1,0:T(8,128)(2,1)} %all-gather.5.cloned.1.call-done, f32[256,1024]{1,0:T(8,128)} %reshape.190, f32[256,1024]{1,0:T(8,128)S(1)} %reshape.188, f32[256,1024]{1,0:T(8,128)} %reshape.189), kind=kOutput, calls=%fused_computation.28 | convolution fusion | flops 538181632 | bytes 6815744 | tf_op jit(solution)/shard_map/dot_general | solution.py:93
  (69 shorter events, 31.9 us)
Async XLA Ops:
  6.5 28.4 %copy-start = (f32[16,127]{1,0:T(8,128)S(1)}, f32[16,127]{1,0:T(8,128)}, u32[]{:S(2)}) copy-start(f32[16,127]{1,0:T(8,128)} %param.9) | copy-start | bytes 24388
  6.5 4.3 %copy-start.2 = (bf16[2,64,1,2,1024]{4,3,2,1,0:T(2,128)(2,1)S(1)}, bf16[2,64,1,2,1024]{4,3,2,1,0:T(2,128)(2,1)}, u32[]{:S(2)}) copy-start(bf16[2,64,1,2,1024]{4,3,2,1,0:T(2,128)(2,1)} %param.6) | copy-start | bytes 1572868
  6.5 115.6 %all-gather.3.cloned.1.call-start = ((), (), s32[]{:S(2)}) async-start(), calls=%async_computation.4 | async-start | bytes 7077888 | tf_op jit(solution)/shard_map/all_gather | solution.py:67
  8.9 23.0 %copy-start.11 = (f32[16,15]{1,0:T(8,128)S(1)}, f32[16,15]{1,0:T(8,128)}, u32[]{:S(2)}) copy-start(f32[16,15]{1,0:T(8,128)} %param.10) | copy-start | bytes 2884
  10.9 22.7 %copy-start.12 = (f32[16,15]{1,0:T(8,128)S(1)}, f32[16,15]{1,0:T(8,128)}, u32[]{:S(2)}) copy-start(f32[16,15]{1,0:T(8,128)} %param.11) | copy-start | bytes 2884
  12.3 13.1 %all-to-all-start.2 = ((bf16[2,64,1,2,1024]{4,3,2,0,1:T(2,128)(2,1)}), bf16[2,64,1,2,1024]{4,3,2,0,1:T(2,128)(2,1)S(1)}, u32[]{:S(2)}, u32[]{:S(2)}) async-start(bf16[2,64,1,2,1024]{4,3,2,0,1:T(2,128)(2,1)} %multiply_convert_fusion), calls=%async_computation.2 | async-start | bytes 1048576 | tf_op jit(solution)/shard_map/all_to_all | solution.py:85
  16.6 185.4 %all-gather.5.cloned.1.call-start = ((), (), s32[]{:S(2)}) async-start(), calls=%async_computation.5 | async-start | bytes 2359296 | tf_op jit(solution)/shard_map/all_gather | solution.py:94
  25.4 34.7 %all-to-all-start = ((bf16[2,64,1,2,1024]{4,3,2,0,1:T(2,128)(2,1)}), bf16[2,64,1,2,1024]{4,3,2,0,1:T(2,128)(2,1)S(1)}, u32[]{:S(2)}, u32[]{:S(2)}) async-start(bf16[2,64,1,2,1024]{4,3,2,0,1:T(2,128)(2,1)} %multiply_convert_fusion), calls=%async_computation | async-start | bytes 1048576 | tf_op jit(solution)/shard_map/all_to_all | solution.py:78
  131.6 2.1 %copy-start.10 = (bf16[256,1024]{1,0:T(8,128)(2,1)S(1)}, bf16[256,1024]{1,0:T(8,128)(2,1)}, u32[]{:S(2)}) copy-start(bf16[256,1024]{1,0:T(8,128)(2,1)} %reshape.181) | copy-start | bytes 1572868
  133.7 5.9 %copy-start.7 = (bf16[2,16,1,8,1,16,64]{6,5,4,3,1,0,2:T(8,128)(2,1)S(1)}, bf16[2,16,1,8,1,16,64]{6,5,4,3,1,0,2:T(8,128)(2,1)}, u32[]{:S(2)}) copy-start(bf16[2,16,1,8,1,16,64]{6,5,4,3,1,0,2:T(8,128)(2,1)} %get-tuple-element.12) | copy-start | bytes 1572868
  133.7 5.9 %copy-start.8 = (bf16[2,16,1,8,1,16,64]{6,5,4,3,1,0,2:T(8,128)(2,1)S(1)}, bf16[2,16,1,8,1,16,64]{6,5,4,3,1,0,2:T(8,128)(2,1)}, u32[]{:S(2)}) copy-start(bf16[2,16,1,8,1,16,64]{6,5,4,3,1,0,2:T(8,128)(2,1)} %get-tuple-element.13) | copy-start | bytes 1572868
  153.0 26.4 %all-to-all-start.3 = ((bf16[2,16,1,8,1024]{4,1,0,2,3:T(8,128)(2,1)}), bf16[2,16,1,8,1024]{4,1,0,2,3:T(8,128)(2,1)}, u32[]{:S(2)}, u32[]{:S(2)}) async-start(bf16[2,16,1,8,1024]{4,1,0,2,3:T(8,128)(2,1)} %reshape.198), calls=%async_computation.3 | async-start | bytes 1048576 | tf_op jit(solution)/shard_map/all_to_all | solution.py:61
  159.6 3.4 %copy-start.9 = (bf16[256,1024]{1,0:T(8,128)(2,1)S(1)}, bf16[256,1024]{1,0:T(8,128)(2,1)}, u32[]{:S(2)}) copy-start(bf16[256,1024]{1,0:T(8,128)(2,1)} %reshape.177) | copy-start | bytes 1572868
  163.0 6.0 %copy-start.6 = (bf16[2,8,8,2,1,16,64]{6,5,4,3,2,1,0:T(8,128)(2,1)S(1)}, bf16[2,8,8,2,1,16,64]{6,5,4,3,2,1,0:T(8,128)(2,1)}, u32[]{:S(2)}) copy-start(bf16[2,8,8,2,1,16,64]{6,5,4,3,2,1,0:T(8,128)(2,1)} %get-tuple-element.5) | copy-start | bytes 1572868
  177.0 6.8 %copy-start.4 = (bf16[2,64,1,2,1,16,64]{6,5,4,3,1,0,2:T(8,128)(2,1)S(1)}, bf16[2,64,1,2,1,16,64]{6,5,4,3,1,0,2:T(8,128)(2,1)}, u32[]{:S(2)}) copy-start(bf16[2,64,1,2,1,16,64]{6,5,4,3,1,0,2:T(8,128)(2,1)} %get-tuple-element.9) | copy-start | bytes 1572868
  177.0 6.8 %copy-start.5 = (bf16[2,64,1,2,1,16,64]{6,5,4,3,1,0,2:T(8,128)(2,1)S(1)}, bf16[2,64,1,2,1,16,64]{6,5,4,3,1,0,2:T(8,128)(2,1)}, u32[]{:S(2)}) copy-start(bf16[2,64,1,2,1,16,64]{6,5,4,3,1,0,2:T(8,128)(2,1)} %get-tuple-element.10) | copy-start | bytes 1572868
  179.4 19.3 %all-to-all-start.1 = ((bf16[2,8,8,2,1024]{4,3,1,0,2:T(2,128)(2,1)}), bf16[2,8,8,2,1024]{4,3,1,0,2:T(2,128)(2,1)}, u32[]{:S(2)}, u32[]{:S(2)}) async-start(bf16[2,8,8,2,1024]{4,3,1,0,2:T(2,128)(2,1)} %reshape.197), calls=%async_computation.1 | async-start | bytes 1048576 | tf_op jit(solution)/shard_map/all_to_all | solution.py:57
  200.2 1.8 copy-start.3
  201.9 4.1 %copy-start.1 = (f32[16,127]{1,0:T(8,128)S(1)}, f32[16,127]{1,0:T(8,128)}, u32[]{:S(2)}) copy-start(f32[16,127]{1,0:T(8,128)} %param.9) | copy-start | bytes 24388
Sparse Core Ops, SparseCore 0:
  9.5 112.5 all-gather.2
  124.3 47.2 all-gather.4
where the time goes:
time: 214 us; the launch traced here: 213 us
  waiting for transfers between devices  88.1 us (41%)
  local copies, waits for them, and re-layouts  42.8 us (20%)
  matrix products  41.5 us (19%)
  starting transfers between devices  19.5 us (9%)
  between operations  13.7 us (6%)
  other arithmetic  7.17 us (3%)
    all_gather x1, waiting for transfers between devices, shards(): gathered = lax.all_gather(w_qkv, 'gy', axis=0, tiled=True)  60.6 us
    all_to_all x1, waiting for transfers between devices, shards(): lax.all_to_all(normed, 'gy', split_axis=1, concat_axis=2, tiled=True)  17.7 us
    dot_general x3, matrix products, project(): jnp.dot(inputs.reshape(-1, features), gathered, preferred_element_type=jn...  17.7 us
    another operation x3, local copies, waits for them, and re-layouts, attend(): parts = qkv.reshape(dims[:-1] + (3, HEADS, HEAD))  10.9 us
    sub x3, matrix products, attend(): scores = scores - jnp.max(scores, axis=-1, keepdims=True)  10.1 us
    all_to_all x1, waiting for transfers between devices, shards(): lax.all_to_all(normed, 'gz', split_axis=1, concat_axis=3, tiled=True)  8.07 us
    dot_general x3, matrix products, attend(): jnp.einsum(mix_form, weights, values, preferred_element_type=jnp.float32)  7.03 us
    all_to_all x1, starting transfers between devices, shards(): lax.all_to_all(normed, 'gy', split_axis=1, concat_axis=2, tiled=True)  6.52 us
  transfers between devices with their start and end apart: 6, of which 4 were waited for; matrix products, arithmetic and copies ran while one was open for 41% of the time, Pallas kernels for 0%

commit v1 on v0

--- a/solution.py
+++ b/solution.py
@@ -1,6 +1,11 @@
+import functools
+
 import jax
 import jax.numpy as jnp
+import numpy as np
 from jax import lax
+from jax.experimental import pallas as pl
+from jax.experimental.pallas import tpu as pltpu
 from jax.sharding import PartitionSpec as P
 
 HEADS = 16
@@ -96,10 +101,337 @@
     return result.astype(jnp.bfloat16).reshape(tokens.shape)
 
 
+def device(**where):
+    return {"device_id": where, "device_id_type": pl.DeviceIdType.MESH}
+
+
+def greet(me_y, me_z, size_y, size_z):
+    barrier = pltpu.get_barrier_semaphore()
+    for step in range(1, size_y):
+        pl.semaphore_signal(barrier, inc=1, **device(gy=lax.rem(me_y + step, size_y)))
+    for step in range(1, size_z):
+        pl.semaphore_signal(barrier, inc=1, **device(gz=lax.rem(me_z + step, size_z)))
+    pl.semaphore_wait(barrier, size_y + size_z - 2)
+
+
+def exchange(source, target, axis, me, size, send_sems, recv_sems):
+    rows = source.shape[1] // size
+    copies = []
+    for step in range(1, size):
+        peer = lax.rem(me + step, size)
+        copies.append(
+            pltpu.make_async_remote_copy(
+                src_ref=source.at[:, pl.ds(pl.multiple_of(peer * rows, rows), rows), :],
+                dst_ref=target.at[:, pl.ds(pl.multiple_of(me * rows, rows), rows), :],
+                send_sem=send_sems.at[step - 1],
+                recv_sem=recv_sems.at[step - 1],
+                **device(**{axis: peer}),
+            )
+        )
+    for copy in copies:
+        copy.start()
+    return copies
+
+
+def keep_own(source, target, me, size):
+    rows = source.shape[1] // size
+    own = pl.ds(pl.multiple_of(me * rows, rows), rows)
+    target[:, own, :] = source[:, own, :]
+
+
+def gather_kernel(
+    size_y, size_z, tokens, w_qkv, w_out, along, all_qkv, all_out,
+    y_send, y_recv, z_send, z_recv, up_send, up_recv, down_send, down_recv,
+    side_send, side_recv, core_send, core_recv, own_sem,
+):
+    me_y, me_z = lax.axis_index("gy"), lax.axis_index("gz")
+    depth = w_qkv.shape[0]
+    half = depth // 2
+    levels = size_y // 2
+    level, side, core = me_y // 2, lax.rem(me_y, 2), lax.rem(me_z, 2)
+    values = tokens[...].astype(jnp.float32)
+    center = jnp.mean(values, axis=-1, keepdims=True)
+    spread = jnp.mean((values - center) ** 2, axis=-1, keepdims=True)
+    along[0] = ((values - center) * lax.rsqrt(spread + 1e-05)).astype(jnp.bfloat16)
+    pairs = ((w_qkv, all_qkv), (w_out, all_out))
+
+    greet(me_y, me_z, size_y, size_z)
+
+    def rows_of(lev, sid):
+        return pl.ds(pl.multiple_of((lev * 2 + sid) * depth + core * half, half), half)
+
+    def transfer(array, lev, sid, sends, recvs, slot, where, own=False):
+        block = pairs[array][1].at[rows_of(lev, sid), :]
+        source = pairs[array][0].at[pl.ds(pl.multiple_of(core * half, half), half), :] if own else block
+        return pltpu.make_async_remote_copy(
+            src_ref=source, dst_ref=block, send_sem=sends.at[array, slot],
+            recv_sem=recvs.at[array, slot], **device(**where),
+        )
+
+    above = {"gy": me_y + 2}
+    below = {"gy": me_y - 2}
+    beside = {"gy": level * 2 + 1 - side}
+    twin = {"gz": me_z + 1 - 2 * core}
+
+    def up(array, step, own=False):
+        return transfer(array, level - step, side, up_send, up_recv, step, above, own)
+
+    def down(array, step, own=False):
+        return transfer(array, level + step, side, down_send, down_recv, step, below, own)
+
+    def across(array, lev, own=False):
+        return transfer(array, lev, side, side_send, side_recv, lev, beside, own)
+
+    def share(array, lev, sid, own=False):
+        return transfer(array, lev, sid, core_send, core_recv, lev * 2 + sid, twin, own)
+
+    sent_y = exchange(along.at[0], along.at[1], "gy", me_y, size_y, y_send, y_recv)
+    sent_z = exchange(along.at[0], along.at[2], "gz", me_z, size_z, z_send, z_recv)
+    for array in (0, 1):
+        pl.when(level + 1 < levels)(lambda: up(array, 0, True).start())
+        pl.when(level > 0)(lambda: down(array, 0, True).start())
+        across(array, level, True).start()
+    own_copies = [
+        pltpu.make_async_copy(
+            pairs[array][0],
+            pairs[array][1].at[pl.ds(pl.multiple_of(me_y * depth, depth), depth), :],
+            own_sem.at[array],
+        )
+        for array in (0, 1)
+    ]
+    for copy in own_copies:
+        copy.start()
+    keep_own(along.at[0], along.at[1], me_y, size_y)
+    keep_own(along.at[0], along.at[2], me_z, size_z)
+    for step in range(levels - 1):
+        for array in (0, 1):
+
+            @pl.when(level - 1 - step >= 0)
+            def _():
+                transfer(array, level - 1 - step, side, up_send, up_recv, step, above).wait_recv()
+                pl.when(level + 1 < levels)(lambda: up(array, step + 1).start())
+                across(array, level - 1 - step).start()
+                share(array, level - 1 - step, side).start()
+
+            @pl.when(level + 1 + step < levels)
+            def _():
+                transfer(array, level + 1 + step, side, down_send, down_recv, step, below).wait_recv()
+                pl.when(level > 0)(lambda: down(array, step + 1).start())
+                across(array, level + 1 + step).start()
+                share(array, level + 1 + step, side).start()
+
+    def finish(copy):
+        copy.wait_send()
+        copy.wait_recv()
+
+    def arrived(array, lev):
+        across_in = transfer(array, lev, 1 - side, side_send, side_recv, lev, beside)
+        across_in.wait_recv()
+        share(array, lev, 1 - side).start()
+
+    for array in (0, 1):
+        arrived(array, level)
+    for step in range(1, levels):
+        for array in (0, 1):
+            pl.when(level - step >= 0)(lambda: arrived(array, level - step))
+            pl.when(level + step < levels)(lambda: arrived(array, level + step))
+
+    for copy in sent_y + sent_z + own_copies:
+        copy.wait()
+    for array in (0, 1):
+        pl.when(level + 1 < levels)(lambda: up(array, 0, True).wait_send())
+        pl.when(level > 0)(lambda: down(array, 0, True).wait_send())
+        across(array, level, True).wait_send()
+        finish(share(array, level, 1 - side))
+        for step in range(1, levels):
+
+            @pl.when(level - step >= 0)
+            def _():
+                pl.when(level + 1 < levels)(lambda: up(array, step).wait_send())
+                across(array, level - step).wait_send()
+                for sid in (side, 1 - side):
+                    finish(share(array, level - step, sid))
+
+            @pl.when(level + step < levels)
+            def _():
+                pl.when(level > 0)(lambda: down(array, step).wait_send())
+                across(array, level + step).wait_send()
+                for sid in (side, 1 - side):
+                    finish(share(array, level + step, sid))
+
+
+def line_places(rows, size_y, size_z, rows_z):
+    row = np.arange(rows)
+    part_y, part_z = rows // size_y, rows // size_z
+    return (
+        (row // rows_z, row % rows_z),
+        (row // part_y, row % part_y),
+        (row // part_z * rows_z + row % rows_z, row % part_z // rows_z),
+    )
+
+
+def offset_lookup(places, lengths, rows):
+    parts, base = [], 0
+    total = sum(2 * length - 1 for length in lengths)
+    for (position, line), length in zip(places, lengths):
+        lookup = np.zeros((total, 2 * rows), np.float32)
+        first, second = np.nonzero(line[:, None] == line[None, :])
+        entry = position[first] - position[second] + length - 1 + base
+        lookup[entry, rows - 1 - first + second] = 1.0
+        parts.append(lookup)
+        base += 2 * length - 1
+    return np.concatenate(parts, axis=1)
+
+
+def attend_kernel(size_y, size_z, rows_z, heads, along, w_q, w_k, w_v, offsets, out):
+    _, samples, rows, features = along.shape
+    wide = w_q.shape[1]
+    tokens = along[...].reshape(3 * samples * rows, features)
+
+    def project(weights):
+        return jnp.dot(tokens, weights[...], preferred_element_type=jnp.float32)
+
+    query = (project(w_q) * HEAD ** (-0.5)).astype(jnp.bfloat16)
+    keys = project(w_k).astype(jnp.bfloat16)
+    values = project(w_v).astype(jnp.bfloat16)
+    row = lax.broadcasted_iota(jnp.int32, (rows, rows), 0)
+    col = lax.broadcasted_iota(jnp.int32, (rows, rows), 1)
+    lane = lax.broadcasted_iota(jnp.int32, (rows, 2 * HEAD), 1)
+    part_y, part_z = rows // size_y, rows // size_z
+    line_of = (
+        lambda r: lax.rem(r, rows_z),
+        lambda r: lax.rem(r, part_y),
+        lambda r: lax.rem(r, part_z) // rows_z,
+    )
+    for axis in range(3):
+        same = line_of[axis](row) == line_of[axis](col)
+        for pair in range(wide // (2 * HEAD)):
+            columns = slice(pair * 2 * HEAD, (pair + 1) * 2 * HEAD)
+            biases = []
+            for half in range(2):
+                entry = offsets[0, pair * 2 + half, axis * 2 * rows : (axis + 1) * 2 * rows]
+                spread = jnp.broadcast_to(entry[None, :], (rows, 2 * rows))
+                spread = pltpu.roll(spread, rows + 1, 1, stride=1, stride_axis=0)
+                biases.append(jnp.where(same, spread[:, :rows], -1e30))
+            for sample in range(samples):
+                first = (axis * samples + sample) * rows
+                part = slice(first, first + rows)
+                mixed = []
+                for half in range(2):
+                    chosen = jnp.where(lane // HEAD == half, query[part, columns], 0)
+                    scores = lax.dot_general(
+                        chosen, keys[part, columns], (((1,), (1,)), ((), ())),
+                        preferred_element_type=jnp.float32,
+                    ) + biases[half]
+                    expo = jnp.exp(scores - jnp.max(scores, axis=-1, keepdims=True))
+                    weights = (expo / jnp.sum(expo, axis=-1, keepdims=True)).astype(jnp.bfloat16)
+                    mixed.append(
+                        jnp.dot(weights, values[part, columns], preferred_element_type=jnp.float32)
+                    )
+                out[axis, sample, :, columns] = jnp.where(lane < HEAD, mixed[0], mixed[1]).astype(
+                    jnp.bfloat16
+                )
+
+
+def return_kernel(
+    size_y, size_z, mixed, tokens, w_out, result, back_y, back_z, y_send, y_recv, z_send, z_recv
+):
+    me_y, me_z = lax.axis_index("gy"), lax.axis_index("gz")
+    greet(me_y, me_z, size_y, size_z)
+    copies = exchange(mixed.at[1], back_y, "gy", me_y, size_y, y_send, y_recv)
+    copies += exchange(mixed.at[2], back_z, "gz", me_z, size_z, z_send, z_recv)
+    keep_own(mixed.at[1], back_y, me_y, size_y)
+    keep_own(mixed.at[2], back_z, me_z, size_z)
+    for copy in copies:
+        copy.wait()
+    summed = mixed[0].astype(jnp.float32) + back_y[...].astype(jnp.float32)
+    summed = (summed + back_z[...].astype(jnp.float32)).astype(jnp.bfloat16)
+    summed = summed.reshape(-1, summed.shape[-1])
+    width = 256
+    for first in range(0, w_out.shape[1], width):
+        columns = slice(first, first + width)
+        product = jnp.dot(summed, w_out[:, columns], preferred_element_type=jnp.float32)
+        residual = tokens[:, :, columns].astype(jnp.float32)
+        result[:, :, columns] = (residual + product.reshape(residual.shape)).astype(jnp.bfloat16)
+
+
+VMEM = pl.BlockSpec(memory_space=pltpu.VMEM)
+ANY = pl.BlockSpec(memory_space=pl.ANY)
+DMA = pltpu.SemaphoreType.DMA
+
+
+def fast_shards(size_y, size_z, tokens, w_qkv, w_out, bias_x, bias_y, bias_z):
+    samples, depth, rows_y, rows_z, features = tokens.shape
+    rows = depth * rows_y * rows_z
+    levels = size_y // 2
+    lengths = [(table.shape[1] + 1) // 2 for table in (bias_x, bias_y, bias_z)]
+    lookup = offset_lookup(line_places(rows, size_y, size_z, rows_z), lengths, rows)
+    offsets = jnp.dot(
+        jnp.concatenate([bias_x, bias_y, bias_z], axis=1), lookup, precision=lax.Precision.HIGHEST
+    )
+    flat = tokens.reshape(samples, rows, features)
+    along, all_qkv, all_out = pl.pallas_call(
+        functools.partial(gather_kernel, size_y, size_z),
+        out_shape=(
+            jax.ShapeDtypeStruct((3, samples, rows, features), jnp.bfloat16),
+            jax.ShapeDtypeStruct((w_qkv.shape[0] * size_y, w_qkv.shape[1]), jnp.bfloat16),
+            jax.ShapeDtypeStruct((w_out.shape[0] * size_y, w_out.shape[1]), jnp.bfloat16),
+        ),
+        in_specs=[VMEM, VMEM, VMEM],
+        out_specs=(VMEM, ANY, ANY),
+        scratch_shapes=[
+            DMA((size_y - 1,)), DMA((size_y - 1,)), DMA((size_z - 1,)), DMA((size_z - 1,)),
+            DMA((2, levels)), DMA((2, levels)), DMA((2, levels)), DMA((2, levels)),
+            DMA((2, levels)), DMA((2, levels)), DMA((2, size_y)), DMA((2, size_y)), DMA((2,)),
+        ],
+        compiler_params=pltpu.CompilerParams(collective_id=0, has_side_effects=True),
+    )(flat, w_qkv, w_out)
+    wide = 4 * HEAD
+    groups = features // wide
+    mixed = pl.pallas_call(
+        functools.partial(attend_kernel, size_y, size_z, rows_z, HEADS),
+        out_shape=jax.ShapeDtypeStruct((3, samples, rows, features), jnp.bfloat16),
+        grid=(groups,),
+        in_specs=[
+            pl.BlockSpec((3, samples, rows, features), lambda g: (0, 0, 0, 0)),
+            pl.BlockSpec((features, wide), lambda g: (0, g)),
+            pl.BlockSpec((features, wide), lambda g: (0, groups + g)),
+            pl.BlockSpec((features, wide), lambda g: (0, 2 * groups + g)),
+            pl.BlockSpec((1, 4, 6 * rows), lambda g: (g, 0, 0)),
+        ],
+        out_specs=pl.BlockSpec((3, samples, rows, wide), lambda g: (0, 0, 0, g)),
+    )(along, all_qkv, all_qkv, all_qkv, offsets.reshape(groups, 4, 6 * rows))
+    result = pl.pallas_call(
+        functools.partial(return_kernel, size_y, size_z),
+        out_shape=jax.ShapeDtypeStruct((samples, rows, features), jnp.bfloat16),
+        in_specs=[VMEM, VMEM, VMEM],
+        out_specs=VMEM,
+        scratch_shapes=[
+            pltpu.VMEM((samples, rows, features), jnp.bfloat16),
+            pltpu.VMEM((samples, rows, features), jnp.bfloat16),
+            DMA((size_y - 1,)), DMA((size_y - 1,)), DMA((size_z - 1,)), DMA((size_z - 1,)),
+        ],
+        compiler_params=pltpu.CompilerParams(collective_id=1, has_side_effects=True),
+    )(mixed, flat, all_out)
+    return result.reshape(tokens.shape)
+
+
+def body_for(size_y, size_z):
+    def body(tokens, *parameters):
+        _, depth, rows_y, rows_z, features = tokens.shape
+        rows = depth * rows_y * rows_z
+        whole_parts = size_y % 2 == 0 and size_z % 2 == 0 and rows == 2 * HEAD
+        if whole_parts and rows_y == 1 and rows % (16 * size_y) == 0 and rows % (16 * size_z) == 0:
+            return fast_shards(size_y, size_z, tokens, *parameters)
+        return shards(tokens, *parameters)
+
+    return body
+
+
 def solution(mesh):
     placed = (P(None, None, "gy", "gz", None), P("gy", None), P("gy", None), P(), P(), P())
     return jax.shard_map(
-        shards,
+        body_for(mesh.shape["gy"], mesh.shape["gz"]),
         mesh=mesh,
         in_specs=placed,
         out_specs=P(None, None, "gy", "gz", None),

time: 214 us -> 131 us (0.61)
  Pallas kernels: 0 us -> 121 us
  waiting for transfers between devices: 88.1 us -> 0 us
  matrix products: 41.5 us -> 3.29 us
  local copies, waits for them, and re-layouts: 42.8 us -> 5.4 us
  starting transfers between devices: 19.5 us -> 0 us
  between operations: 13.7 us -> 0.04 us
  other arithmetic: 7.17 us -> 0 us
    pallas_call x0 -> x3, Pallas kernels: none -> 121 us  [the longest x1 64.6 us: fast_shards(): pl.pallas_call(functools.partial(gather_kernel, size_y, size_z), out_shap...]
    all_gather x2 -> x0, waiting for transfers between devices: 60.6 us -> none  [the longest x1 60.6 us: shards(): gathered = lax.all_gather(w_qkv, 'gy', axis=0, tiled=True)]
    dot_general x10 -> x3, matrix products: 31.4 us -> 3.29 us  [fast_shards(): jnp.dot(jnp.concatenate([bias_x, bias_y, bias_z], axis=1), lookup, precis...]
    all_to_all x4 -> x0, waiting for transfers between devices: 26.1 us -> none  [the longest x1 17.7 us: shards(): lax.all_to_all(normed, 'gy', split_axis=1, concat_axis=2, tiled=True)]
    all_to_all x4 -> x0, starting transfers between devices: 19.5 us -> none  [the longest x1 6.52 us: shards(): lax.all_to_all(normed, 'gy', split_axis=1, concat_axis=2, tiled=True)]
    convert_element_type x13 -> x0, local copies, waits for them, and re-layouts: 16.7 us -> none  [the longest x4 5.45 us: attend(): return mixed.reshape(dims[:-1] + (features,)).astype(jnp.bfloat16)]
    another operation x3 -> x0, local copies, waits for them, and re-layouts: 10.9 us -> none  [attend(): parts = qkv.reshape(dims[:-1] + (3, HEADS, HEAD))]
    sub x3 -> x0, matrix products: 10.1 us -> none  [attend(): scores = scores - jnp.max(scores, axis=-1, keepdims=True)]
  transfers between devices with their start and end apart: 6 -> 0, of which waited for: 4 -> 0; matrix products, arithmetic and copies ran while one was open for 41% -> 0% of each run, Pallas kernels for 0% -> 0%
where the time goes in v1:
time: 131 us; the launch traced here: 129 us
  Pallas kernels  121 us (92%)
  local copies, waits for them, and re-layouts  5.4 us (4%)
  matrix products  3.29 us (3%)
    pallas_call x1, Pallas kernels, fast_shards(): pl.pallas_call(functools.partial(gather_kernel, size_y, size_z), out_shap...  64.6 us
    pallas_call x1, Pallas kernels, fast_shards(): pl.pallas_call(functools.partial(attend_kernel, size_y, size_z, rows_z, H...  38.6 us
    pallas_call x1, Pallas kernels, fast_shards(): pl.pallas_call(functools.partial(return_kernel, size_y, size_z), out_shap...  17.5 us
    dot_general x3, matrix products, fast_shards(): jnp.dot(jnp.concatenate([bias_x, bias_y, bias_z], axis=1), lookup, precis...  3.29 us

profile of v1, /device:TPU:0, one launch (start us, length us, event | category | flops | bytes accessed | tf_op | source)
XLA Modules:
  0.0 129.5 jit_solution(15918085780778262929)
XLA Ops:
  0.0 0.0 copy-start
  0.0 0.7 copy-done
  0.7 1.3 %fusion.1 = f32[768,16]{0,1:T(8,128)S(1)} fusion(f32[127,768]{1,0:T(8,128)} %constant.4, f32[16,127]{1,0:T(8,128)S(1)} %copy-done), kind=kOutput, calls=%fused_computation.3 | convolution fusion | flops 18726912 | bytes 447424 | tf_op jit(solution)/shard_map/dot_general | solution.py:369
  2.0 1.0 convolution_add_fusion.1
  3.0 1.0 fusion
  4.0 0.6 reshape.10.offsets
  4.6 2.0 %reshape.9.tokens = bf16[2,128,1024]{2,1,0:T(8,128)(2,1)} reshape(bf16[2,64,1,2,1024]{4,3,2,1,0:T(2,128)(2,1)} %param.7) | data formatting | bytes 1048576 | tf_op jit(solution)/shard_map/reshape | solution.py:372
  6.7 64.6 %shard_map.73 = (bf16[3,2,128,1024]{3,2,1,0:T(8,128)(2,1)}, bf16[1024,3072]{1,0:T(8,128)(2,1)}, bf16[1024,1024]{1,0:T(8,128)(2,1)}) custom-call(bf16[2,128,1024]{2,1,0:T(8,128)(2,1)} %reshape.9.tokens, bf16[128,3072]{1,0:T(8,128)(2,1)} %w_qkv.1, bf16[128,1024]{1,0:T(8,128)(2,1)} %w_out.1), custom_call_target="tpu_custom_call" | custom-call | tf_op jit(solution)/shard_map/pallas_call | solution.py:373
  71.3 38.6 %shard_map.74.mixed = bf16[3,2,128,1024]{3,2,1,0:T(8,128)(2,1)} custom-call(bf16[3,2,128,1024]{3,2,1,0:T(8,128)(2,1)} %get-tuple-element.8.along, bf16[1024,3072]{1,0:T(8,128)(2,1)} %get-tuple-element.9.w_q.w_k.w_v, bf16[1024,3072]{1,0:T(8,128)(2,1)} %get-tuple-element.9.w_q.w_k.w_v, bf16[1024,3072]{1,0:T(8,128)(2,1)} %get-tuple-element.9.w_q.w_k.w_v, ...), custom_call_target="tpu_custom_call" | custom-call | tf_op jit(solution)/shard_map/pallas_call | solution.py:391
  109.9 17.5 %shard_map.75 = bf16[2,128,1024]{2,1,0:T(8,128)(2,1)} custom-call(bf16[3,2,128,1024]{3,2,1,0:T(8,128)(2,1)} %shard_map.74.mixed, bf16[2,128,1024]{2,1,0:T(8,128)(2,1)} %reshape.9.tokens, bf16[1024,1024]{1,0:T(8,128)(2,1)} %get-tuple-element.10.w_out), custom_call_target="tpu_custom_call" | custom-call | tf_op jit(solution)/shard_map/pallas_call | solution.py:404
  127.4 2.0 %reshape.11 = bf16[2,64,1,2,1024]{4,3,1,0,2:T(2,128)(2,1)} reshape(bf16[2,128,1024]{2,1,0:T(8,128)(2,1)} %shard_map.75) | data formatting | bytes 1048576 | tf_op jit(solution)/shard_map/reshape | solution.py:416
Async XLA Ops:
  0.0 0.7 copy-start

commit v2 on v0

--- a/solution.py
+++ b/solution.py
@@ -1,6 +1,11 @@
+import functools
+
 import jax
 import jax.numpy as jnp
+import numpy as np
 from jax import lax
+from jax.experimental import pallas as pl
+from jax.experimental.pallas import tpu as pltpu
 from jax.sharding import PartitionSpec as P
 
 HEADS = 16
@@ -96,10 +101,440 @@
     return result.astype(jnp.bfloat16).reshape(tokens.shape)
 
 
+def device(**where):
+    return {"device_id": where, "device_id_type": pl.DeviceIdType.MESH}
+
+
+def greet(me_y, me_z, size_y, size_z):
+    barrier = pltpu.get_barrier_semaphore()
+    for step in range(1, size_y):
+        pl.semaphore_signal(barrier, inc=1, **device(gy=lax.rem(me_y + step, size_y)))
+    for step in range(1, size_z):
+        pl.semaphore_signal(barrier, inc=1, **device(gz=lax.rem(me_z + step, size_z)))
+    pl.semaphore_wait(barrier, size_y + size_z - 2)
+
+
+def exchange(source, target, axis, me, size, send_sems, recv_sems):
+    rows = source.shape[1] // size
+    copies = []
+    for step in range(1, size):
+        peer = lax.rem(me + step, size)
+        copies.append(
+            pltpu.make_async_remote_copy(
+                src_ref=source.at[:, pl.ds(pl.multiple_of(peer * rows, rows), rows), :],
+                dst_ref=target.at[:, pl.ds(pl.multiple_of(me * rows, rows), rows), :],
+                send_sem=send_sems.at[step - 1],
+                recv_sem=recv_sems.at[step - 1],
+                **device(**{axis: peer}),
+            )
+        )
+    for copy in copies:
+        copy.start()
+    return copies
+
+
+def keep_own(source, target, me, size):
+    rows = source.shape[1] // size
+    own = pl.ds(pl.multiple_of(me * rows, rows), rows)
+    target[:, own, :] = source[:, own, :]
+
+
+def line_places(rows, size_y, size_z, rows_z):
+    row = np.arange(rows)
+    part_y, part_z = rows // size_y, rows // size_z
+    return (
+        (row // rows_z, row % rows_z),
+        (row // part_y, row % part_y),
+        (row // part_z * rows_z + row % rows_z, row % part_z // rows_z),
+    )
+
+
+def offset_lookup(places, lengths, rows):
+    parts, base = [], 0
+    total = sum(2 * length - 1 for length in lengths)
+    for (position, line), length in zip(places, lengths):
+        lookup = np.zeros((total, 2 * rows), np.float32)
+        first, second = np.nonzero(line[:, None] == line[None, :])
+        entry = position[first] - position[second] + length - 1 + base
+        lookup[entry, rows - 1 - first + second] = 1.0
+        parts.append(lookup)
+        base += 2 * length - 1
+    return np.concatenate(parts, axis=1)
+
+
+def fused_kernel(
+    size_y, size_z, rows_z, tokens, weights, offsets, result,
+    along, full, biases, mixed, back_y, back_z,
+    y_send, y_recv, z_send, z_recv, up_send, up_recv, down_send, down_recv,
+    side_send, side_recv, far_send, far_recv, core_send, core_recv, twin_send, twin_recv,
+    ry_send, ry_recv, rz_send, rz_recv,
+):
+    me_y, me_z = lax.axis_index("gy"), lax.axis_index("gz")
+    samples, rows, features = tokens.shape
+    depth = weights.shape[1]
+    half = depth // 2
+    quarter = half // 4
+    levels = size_y // 2
+    wide = 4 * HEAD
+    groups = features // wide
+    level, side, core = me_y // 2, lax.rem(me_y, 2), lax.rem(me_z, 2)
+    flank = lax.rem(me_z // 2, 2)
+    above, below = {"gy": me_y + 2}, {"gy": me_y - 2}
+    beside = {"gy": level * 2 + 1 - side}
+    twin = {"gz": me_z + 1 - 2 * core}
+    far = {"gz": me_z + 2 - 4 * flank}
+
+    values = tokens[...].astype(jnp.float32)
+    center = jnp.mean(values, axis=-1, keepdims=True)
+    spread = jnp.mean((values - center) ** 2, axis=-1, keepdims=True)
+    along[0] = ((values - center) * lax.rsqrt(spread + 1e-05)).astype(jnp.bfloat16)
+
+    greet(me_y, me_z, size_y, size_z)
+
+    def columns_of(group):
+        return pl.ds(pl.multiple_of(group * wide, wide), wide)
+
+    def transfer(group, lev, sid, start, count, sends, recvs, slot, where, own=False):
+        first = core * half + start
+        cols = columns_of(group)
+        block = full.at[
+            :, pl.ds(pl.multiple_of((lev * 2 + sid) * depth + first, quarter), count), cols
+        ]
+        source = block
+        if own:
+            source = weights.at[:, pl.ds(pl.multiple_of(first, quarter), count), cols]
+        return pltpu.make_async_remote_copy(
+            src_ref=source, dst_ref=block, send_sem=sends.at[group, slot],
+            recv_sem=recvs.at[group, slot], **device(**where),
+        )
+
+    mine, held = flank * quarter, 3 * quarter
+
+    def up(group, step, own=False):
+        return transfer(group, level - step, side, mine, held, up_send, up_recv, step, above, own)
+
+    def up_in(group, step):
+        return transfer(group, level - 1 - step, side, mine, held, up_send, up_recv, step, above)
+
+    def down(group, step, own=False):
+        return transfer(group, level + step, side, mine, held, down_send, down_recv, step, below, own)
+
+    def down_in(group, step):
+        return transfer(group, level + 1 + step, side, mine, held, down_send, down_recv, step, below)
+
+    def across(group, lev, own=False):
+        return transfer(group, lev, side, mine, held, side_send, side_recv, lev, beside, own)
+
+    def across_in(group, lev):
+        return transfer(group, lev, 1 - side, mine, held, side_send, side_recv, lev, beside)
+
+    def share(group, lev, sid):
+        return transfer(
+            group, lev, sid, mine, held, core_send, core_recv, lev * 2 + sid, twin
+        )
+
+    def to_far(group, lev, sid):
+        return transfer(
+            group, lev, sid, flank * 3 * quarter, quarter, far_send, far_recv, lev * 2 + sid, far
+        )
+
+    def share_far(group, lev, sid):
+        return transfer(
+            group, lev, sid, (1 - flank) * 3 * quarter, quarter,
+            twin_send, twin_recv, lev * 2 + sid, twin,
+        )
+
+    def own_blocks(group):
+        pl.when(level + 1 < levels)(lambda: up(group, 0, True).start())
+        pl.when(level > 0)(lambda: down(group, 0, True).start())
+        across(group, level, True).start()
+
+    def spread_block(group, lev, sid):
+        to_far(group, lev, sid).start()
+        share(group, lev, sid).start()
+
+    def chain(group, step):
+        @pl.when(level - 1 - step >= 0)
+        def _():
+            up_in(group, step).wait_recv()
+            pl.when(level + 1 < levels)(lambda: up(group, step + 1).start())
+            across(group, level - 1 - step).start()
+            spread_block(group, level - 1 - step, side)
+
+        @pl.when(level + 1 + step < levels)
+        def _():
+            down_in(group, step).wait_recv()
+            pl.when(level > 0)(lambda: down(group, step + 1).start())
+            across(group, level + 1 + step).start()
+            spread_block(group, level + 1 + step, side)
+
+    def from_side(group, step):
+        def arrived(lev):
+            across_in(group, lev).wait_recv()
+            spread_block(group, lev, 1 - side)
+
+        if step == 0:
+            arrived(level)
+        else:
+            pl.when(level - step >= 0)(lambda: arrived(level - step))
+            pl.when(level + step < levels)(lambda: arrived(level + step))
+
+    def each_block(act):
+        act(level, 1 - side)
+        for step in range(1, levels):
+            for lev, there in ((level - step, level - step >= 0), (level + step, level + step < levels)):
+
+                @pl.when(there)
+                def _():
+                    act(lev, side)
+                    act(lev, 1 - side)
+
+    def from_far(group):
+        def act(lev, sid):
+            to_far_in = transfer(
+                group, lev, sid, (1 - flank) * 3 * quarter, quarter,
+                far_send, far_recv, lev * 2 + sid, far,
+            )
+            to_far_in.wait_recv()
+            share_far(group, lev, sid).start()
+
+        each_block(act)
+
+    def complete(group):
+        def act(lev, sid):
+            transfer(
+                group, lev, sid, mine, held, core_send, core_recv, lev * 2 + sid, twin
+            ).wait_recv()
+            share_far(group, lev, sid).wait_recv()
+
+        each_block(act)
+
+    def drain(group):
+        pl.when(level + 1 < levels)(lambda: up(group, 0, True).wait_send())
+        pl.when(level > 0)(lambda: down(group, 0, True).wait_send())
+        across(group, level, True).wait_send()
+        for step in range(1, levels):
+
+            @pl.when(level - step >= 0)
+            def _():
+                pl.when(level + 1 < levels)(lambda: up(group, step).wait_send())
+                across(group, level - step).wait_send()
+
+            @pl.when(level + step < levels)
+            def _():
+                pl.when(level > 0)(lambda: down(group, step).wait_send())
+                across(group, level + step).wait_send()
+
+        def act(lev, sid):
+            to_far(group, lev, sid).wait_send()
+            share(group, lev, sid).wait_send()
+            share_far(group, lev, sid).wait_send()
+
+        each_block(act)
+
+    own_blocks(0)
+    sent_y = exchange(along.at[0], along.at[1], "gy", me_y, size_y, y_send, y_recv)
+    sent_z = exchange(along.at[0], along.at[2], "gz", me_z, size_z, z_send, z_recv)
+    own_blocks(1)
+    full[:, pl.ds(pl.multiple_of(me_y * depth, depth), depth), :] = weights[...]
+    keep_own(along.at[0], along.at[1], me_y, size_y)
+    keep_own(along.at[0], along.at[2], me_z, size_z)
+
+    for step in range(levels - 1):
+        chain(0, step)
+
+    row = lax.broadcasted_iota(jnp.int32, (rows, rows), 0)
+    col = lax.broadcasted_iota(jnp.int32, (rows, rows), 1)
+    lane = lax.broadcasted_iota(jnp.int32, (rows, 2 * HEAD), 1)
+    part_y, part_z = rows // size_y, rows // size_z
+    line_of = (
+        lambda r: lax.rem(r, rows_z),
+        lambda r: lax.rem(r, part_y),
+        lambda r: lax.rem(r, part_z) // rows_z,
+    )
+
+    def fill_bias(group, carry):
+        for axis in range(3):
+            same = line_of[axis](row) == line_of[axis](col)
+            for head in range(4):
+                entry = offsets[group, head, axis * 2 * rows : (axis + 1) * 2 * rows]
+                table = jnp.broadcast_to(entry[None, :], (rows, 2 * rows))
+                table = pltpu.roll(table, rows + 1, 1, stride=1, stride_axis=0)
+                biases[axis, group * 4 + head] = jnp.where(same, table[:, :rows], -1e30)
+        return carry
+
+    lax.fori_loop(0, groups, fill_bias, 0)
+
+    for step in range(levels):
+        from_side(0, step)
+    for copy in sent_y + sent_z:
+        copy.wait()
+    from_far(0)
+    complete(0)
+
+    def attend(group, axis, pair, query, keys, contents):
+        cols = slice(pair * 2 * HEAD, (pair + 1) * 2 * HEAD)
+        for sample in range(samples):
+            first = (axis * samples + sample) * rows
+            part = slice(first, first + rows)
+            outs = []
+            for odd in range(2):
+                chosen = jnp.where(lane // HEAD == odd, query[part, cols], 0)
+                scores = lax.dot_general(
+                    chosen, keys[part, cols], (((1,), (1,)), ((), ())),
+                    preferred_element_type=jnp.float32,
+                ) + biases[axis, group * 4 + pair * 2 + odd]
+                expo = jnp.exp(scores - jnp.max(scores, axis=-1, keepdims=True))
+                scale = 1.0 / jnp.sum(expo, axis=-1, keepdims=True)
+                outs.append(
+                    jnp.dot(
+                        (expo * scale).astype(jnp.bfloat16), contents[part, cols],
+                        preferred_element_type=jnp.float32,
+                    )
+                )
+            place = pl.ds(pl.multiple_of(group * wide + pair * 2 * HEAD, 2 * HEAD), 2 * HEAD)
+            mixed[axis, sample, :, place] = jnp.where(lane < HEAD, outs[0], outs[1]).astype(
+                jnp.bfloat16
+            )
+
+    def returns(group):
+        cols = columns_of(group)
+        there = [
+            (mixed.at[1], back_y, "gy", me_y, size_y, ry_send, ry_recv),
+            (mixed.at[2], back_z, "gz", me_z, size_z, rz_send, rz_recv),
+        ]
+        copies = []
+        for source, target, axis, me, size, sends, recvs in there:
+            count = rows // size
+            for step in range(1, size):
+                peer = lax.rem(me + step, size)
+                copies.append(
+                    pltpu.make_async_remote_copy(
+                        src_ref=source.at[:, pl.ds(pl.multiple_of(peer * count, count), count), cols],
+                        dst_ref=target.at[:, pl.ds(pl.multiple_of(me * count, count), count), cols],
+                        send_sem=sends.at[group, step - 1],
+                        recv_sem=recvs.at[group, step - 1],
+                        **device(**{axis: peer}),
+                    )
+                )
+        return copies
+
+    def group_step(group, carry):
+        ahead = group + 1
+        more = ahead < groups
+        flat = along[...].reshape(3 * samples * rows, features)
+        cols = columns_of(group)
+
+        def project(which):
+            return jnp.dot(flat, full[which, :, cols], preferred_element_type=jnp.float32)
+
+        pl.when(more)(lambda: chain(ahead, 0))
+        query = (project(0) * HEAD ** (-0.5)).astype(jnp.bfloat16)
+        keys = project(1).astype(jnp.bfloat16)
+        contents = project(2).astype(jnp.bfloat16)
+        pl.when(ahead + 1 < groups)(lambda: own_blocks(ahead + 1))
+        pending = [functools.partial(chain, ahead, step) for step in range(1, levels - 1)]
+        pending += [functools.partial(from_side, ahead, step) for step in range(levels)]
+        pieces = [(axis, pair) for axis in (1, 2, 0) for pair in range(wide // (2 * HEAD))]
+        for number, (axis, pair) in enumerate(pieces):
+            attend(group, axis, pair, query, keys, contents)
+            if number < len(pending):
+                now = [pending[number]] if number + 1 < len(pieces) else pending[number:]
+
+                @pl.when(more)
+                def _():
+                    for act in now:
+                        act()
+
+        for copy in returns(group):
+            copy.start()
+
+        @pl.when(more)
+        def _():
+            from_far(ahead)
+            complete(ahead)
+
+        return carry
+
+    lax.fori_loop(0, groups, group_step, 0)
+    keep_own(mixed.at[1], back_y, me_y, size_y)
+    keep_own(mixed.at[2], back_z, me_z, size_z)
+
+    def finish(group, carry):
+        drain(group)
+        for copy in returns(group):
+            copy.wait()
+        return carry
+
+    lax.fori_loop(0, groups, finish, 0)
+    summed = mixed[0].astype(jnp.float32) + back_y[...].astype(jnp.float32)
+    summed = (summed + back_z[...].astype(jnp.float32)).astype(jnp.bfloat16)
+    summed = summed.reshape(-1, features)
+    for first in range(0, features, wide):
+        cols = slice(first, first + wide)
+        product = jnp.dot(summed, full[3, :, cols], preferred_element_type=jnp.float32)
+        residual = tokens[:, :, cols].astype(jnp.float32)
+        result[:, :, cols] = (residual + product.reshape(residual.shape)).astype(jnp.bfloat16)
+
+
+VMEM = pl.BlockSpec(memory_space=pltpu.VMEM)
+DMA = pltpu.SemaphoreType.DMA
+
+
+def fast_shards(size_y, size_z, tokens, w_qkv, w_out, bias_x, bias_y, bias_z):
+    samples, depth, rows_y, rows_z, features = tokens.shape
+    rows = depth * rows_y * rows_z
+    levels = size_y // 2
+    groups = features // (4 * HEAD)
+    lengths = [(table.shape[1] + 1) // 2 for table in (bias_x, bias_y, bias_z)]
+    lookup = offset_lookup(line_places(rows, size_y, size_z, rows_z), lengths, rows)
+    offsets = jnp.dot(
+        jnp.concatenate([bias_x, bias_y, bias_z], axis=1), lookup, precision=lax.Precision.HIGHEST
+    )
+    weights = jnp.stack([w_qkv[:, n * features : (n + 1) * features] for n in range(3)] + [w_out])
+    block = (samples, rows, features)
+    result = pl.pallas_call(
+        functools.partial(fused_kernel, size_y, size_z, rows_z),
+        out_shape=jax.ShapeDtypeStruct(block, jnp.bfloat16),
+        in_specs=[VMEM, VMEM, VMEM],
+        out_specs=VMEM,
+        scratch_shapes=[
+            pltpu.VMEM((3,) + block, jnp.bfloat16),
+            pltpu.VMEM((4, features, features), jnp.bfloat16),
+            pltpu.VMEM((3, HEADS, rows, rows), jnp.float32),
+            pltpu.VMEM((3,) + block, jnp.bfloat16),
+            pltpu.VMEM(block, jnp.bfloat16),
+            pltpu.VMEM(block, jnp.bfloat16),
+            DMA((size_y - 1,)), DMA((size_y - 1,)), DMA((size_z - 1,)), DMA((size_z - 1,)),
+            DMA((groups, levels)), DMA((groups, levels)), DMA((groups, levels)), DMA((groups, levels)),
+            DMA((groups, levels)), DMA((groups, levels)),
+            DMA((groups, size_y)), DMA((groups, size_y)),
+            DMA((groups, size_y)), DMA((groups, size_y)),
+            DMA((groups, size_y)), DMA((groups, size_y)),
+            DMA((groups, size_y - 1)), DMA((groups, size_y - 1)),
+            DMA((groups, size_z - 1)), DMA((groups, size_z - 1)),
+        ],
+        compiler_params=pltpu.CompilerParams(collective_id=0, has_side_effects=True),
+    )(tokens.reshape(block), weights, offsets.reshape(groups, 4, 6 * rows))
+    return result.reshape(tokens.shape)
+
+
+def body_for(size_y, size_z):
+    def body(tokens, *parameters):
+        _, depth, rows_y, rows_z, features = tokens.shape
+        rows = depth * rows_y * rows_z
+        whole_parts = size_y % 2 == 0 and size_z % 4 == 0 and rows == 2 * HEAD
+        if whole_parts and rows_y == 1 and rows % (16 * size_y) == 0 and rows % (16 * size_z) == 0:
+            return fast_shards(size_y, size_z, tokens, *parameters)
+        return shards(tokens, *parameters)
+
+    return body
+
+
 def solution(mesh):
     placed = (P(None, None, "gy", "gz", None), P("gy", None), P("gy", None), P(), P(), P())
     return jax.shard_map(
-        shards,
+        body_for(mesh.shape["gy"], mesh.shape["gz"]),
         mesh=mesh,
         in_specs=placed,
         out_specs=P(None, None, "gy", "gz", None),

time: 214 us -> 108 us (0.50)
  Pallas kernels: 0 us -> 100 us
  waiting for transfers between devices: 88.1 us -> 0 us
  matrix products: 41.5 us -> 0.69 us
  local copies, waits for them, and re-layouts: 42.8 us -> 5.96 us
  starting transfers between devices: 19.5 us -> 0 us
  between operations: 13.7 us -> 0.07 us
  other arithmetic: 7.17 us -> 1.1 us
    pallas_call x0 -> x1, Pallas kernels: none -> 100 us  [fast_shards(): pl.pallas_call(functools.partial(fused_kernel, size_y, size_z, rows_z), o...]
    all_gather x2 -> x0, waiting for transfers between devices: 60.6 us -> none  [the longest x1 60.6 us: shards(): gathered = lax.all_gather(w_qkv, 'gy', axis=0, tiled=True)]
    dot_general x10 -> x3, matrix products: 31.4 us -> 0.69 us  [fast_shards(): jnp.dot(jnp.concatenate([bias_x, bias_y, bias_z], axis=1), lookup, precis...]
    all_to_all x4 -> x0, waiting for transfers between devices: 26.1 us -> none  [the longest x1 17.7 us: shards(): lax.all_to_all(normed, 'gy', split_axis=1, concat_axis=2, tiled=True)]
    all_to_all x4 -> x0, starting transfers between devices: 19.5 us -> none  [the longest x1 6.52 us: shards(): lax.all_to_all(normed, 'gy', split_axis=1, concat_axis=2, tiled=True)]
    convert_element_type x13 -> x0, local copies, waits for them, and re-layouts: 16.7 us -> none  [the longest x4 5.45 us: attend(): return mixed.reshape(dims[:-1] + (features,)).astype(jnp.bfloat16)]
    sub x3 -> x0, matrix products: 10.1 us -> none  [attend(): scores = scores - jnp.max(scores, axis=-1, keepdims=True)]
    another operation x3 -> x1, local copies, waits for them, and re-layouts: 10.9 us -> 1.2 us  [fast_shards(): jnp.stack([w_qkv[:, n * features:(n + 1) * features] for n in range(3)] +...]
  transfers between devices with their start and end apart: 6 -> 0, of which waited for: 4 -> 0; matrix products, arithmetic and copies ran while one was open for 41% -> 0% of each run, Pallas kernels for 0% -> 0%
where the time goes in v2:
time: 108 us
  Pallas kernels  100 us (93%)
  local copies, waits for them, and re-layouts  5.96 us (6%)
  other arithmetic  1.1 us (1%)
    pallas_call x1, Pallas kernels, fast_shards(): pl.pallas_call(functools.partial(fused_kernel, size_y, size_z, rows_z), o...  100 us

profile of v2, /device:TPU:0, one launch (start us, length us, event | category | flops | bytes accessed | tf_op | source)
XLA Modules:
  0.0 108.1 jit_solution(8283563266857881232)
XLA Ops:
  0.0 0.0 copy-start
  0.0 0.0 copy-start.3
  0.0 1.2 %slice_bitcast_fusion.2 = (bf16[1,128,1024]{2,1,0:T(8,128)(2,1)S(1)}, bf16[1,128,1024]{2,1,0:T(8,128)(2,1)S(1)}, bf16[1,128,1024]{2,1,0:T(8,128)(2,1)S(1)}) fusion(bf16[128,3072]{1,0:T(8,128)(2,1)} %param.8), kind=kLoop, calls=%fused_computation.6 | loop fusion | bytes 1572864 | tf_op jit(solution)/shard_map/stack | solution.py:494
  1.2 0.0 copy-done.3
  1.2 0.0 copy-start.1
  1.2 1.1 %pad_maximum_fusion.weights = bf16[4,128,1024]{2,1,0:T(8,128)(2,1)} fusion(bf16[1,128,1024]{2,1,0:T(8,128)(2,1)S(1)} %bitcast.16, bf16[1,128,1024]{2,1,0:T(8,128)(2,1)S(1)} %get-tuple-element.6, bf16[1,128,1024]{2,1,0:T(8,128)(2,1)S(1)} %get-tuple-element.7, bf16[1,128,1024]{2,1,0:T(8,128)(2,1)S(1)} %get-tuple-element.5), kind=kLoop, calls=%fused_computation.3 | loop fusion | flops 1572864 | bytes 2097152 | tf_op jit(solution)/shard_map/stack | solution.py:494
  2.3 0.0 copy-done.1
  2.3 0.0 copy-start.2
  2.3 1.0 reshape.9.tokens
  3.3 0.0 copy-done
  3.3 0.0 copy-done.2
  3.3 0.0 copy-start.5
  3.3 0.3 fusion.1
  3.7 0.5 copy-done.5
  4.1 0.0 copy-done.6
  4.1 0.0 copy-start.4
  4.1 0.0 copy-start.7
  4.1 0.2 convolution_add_fusion.1
  4.3 0.6 copy-done.4
  4.9 0.0 copy-done.7
  4.9 0.2 fusion
  5.1 0.6 reshape.10.offsets
  5.8 100.3 %shard_map.73 = bf16[2,128,1024]{2,1,0:T(8,128)(2,1)} custom-call(bf16[2,128,1024]{2,1,0:T(8,128)(2,1)} %reshape.9.tokens, bf16[4,128,1024]{2,1,0:T(8,128)(2,1)} %pad_maximum_fusion.weights, f32[4,4,768]{2,1,0:T(4,128)} %reshape.10.offsets), custom_call_target="tpu_custom_call" | custom-call | tf_op jit(solution)/shard_map/pallas_call | solution.py:496
  106.1 2.0 %reshape.11 = bf16[2,64,1,2,1024]{4,3,1,0,2:T(2,128)(2,1)} reshape(bf16[2,128,1024]{2,1,0:T(8,128)(2,1)} %shard_map.73) | data formatting | bytes 1048576 | tf_op jit(solution)/shard_map/reshape | solution.py:519
  (1 shorter events, 0.0 us)
Async XLA Ops:
  0.0 3.3 %copy-start = (f32[16,127]{1,0:T(8,128)S(1)}, f32[16,127]{1,0:T(8,128)}, u32[]{:S(2)}) copy-start(f32[16,127]{1,0:T(8,128)} %param.10) | copy-start | bytes 24388
  0.0 1.2 %copy-start.3 = (bf16[128,1024]{1,0:T(8,128)(2,1)S(1)}, bf16[128,1024]{1,0:T(8,128)(2,1)}, u32[]{:S(2)}) copy-start(bf16[128,1024]{1,0:T(8,128)(2,1)} %param.9) | copy-start | bytes 786436
  1.2 1.1 %copy-start.1 = (bf16[2,64,1,2,1024]{4,3,2,1,0:T(2,128)(2,1)S(1)}, bf16[2,64,1,2,1024]{4,3,2,1,0:T(2,128)(2,1)}, u32[]{:S(2)}) copy-start(bf16[2,64,1,2,1024]{4,3,2,1,0:T(2,128)(2,1)} %param.7) | copy-start | bytes 1572868
  2.3 1.0 copy-start.2
  3.3 0.8 copy-start.5
  3.3 0.8 copy-start.6
  4.1 0.8 copy-start.4
  4.1 0.8 copy-start.7

commit v3 on v2

--- a/solution.py
+++ b/solution.py
@@ -335,13 +335,11 @@
     own_blocks(0)
     sent_y = exchange(along.at[0], along.at[1], "gy", me_y, size_y, y_send, y_recv)
     sent_z = exchange(along.at[0], along.at[2], "gz", me_z, size_z, z_send, z_recv)
-    own_blocks(1)
+    for group in range(1, groups):
+        own_blocks(group)
     full[:, pl.ds(pl.multiple_of(me_y * depth, depth), depth), :] = weights[...]
     keep_own(along.at[0], along.at[1], me_y, size_y)
     keep_own(along.at[0], along.at[2], me_z, size_z)
-
-    for step in range(levels - 1):
-        chain(0, step)
 
     row = lax.broadcasted_iota(jnp.int32, (rows, rows), 0)
     col = lax.broadcasted_iota(jnp.int32, (rows, rows), 1)
@@ -365,37 +363,62 @@
 
     lax.fori_loop(0, groups, fill_bias, 0)
 
+    hops = levels - 1
+    waves = [
+        [(wave - step, step) for step in range(hops) if 0 <= wave - step < groups]
+        for wave in range(groups + hops - 1)
+    ]
+
+    def run(chosen):
+        for wave in chosen:
+            for group, step in wave:
+                chain(group, step)
+
+    run(waves[:hops])
     for step in range(levels):
         from_side(0, step)
+    run(waves[hops : hops + 1])
+    from_far(0)
+    if groups > 1:
+        for step in range(levels):
+            from_side(1, step)
+    run(waves[hops + 1 : -1])
     for copy in sent_y + sent_z:
         copy.wait()
-    from_far(0)
     complete(0)
 
-    def attend(group, axis, pair, query, keys, contents):
-        cols = slice(pair * 2 * HEAD, (pair + 1) * 2 * HEAD)
-        for sample in range(samples):
+    def attend(group, axis, query, keys, contents):
+        units = [
+            (pair, sample, odd)
+            for pair in range(wide // (2 * HEAD)) for sample in range(samples) for odd in range(2)
+        ]
+
+        def parts(pair, sample):
             first = (axis * samples + sample) * rows
-            part = slice(first, first + rows)
-            outs = []
-            for odd in range(2):
-                chosen = jnp.where(lane // HEAD == odd, query[part, cols], 0)
-                scores = lax.dot_general(
-                    chosen, keys[part, cols], (((1,), (1,)), ((), ())),
-                    preferred_element_type=jnp.float32,
-                ) + biases[axis, group * 4 + pair * 2 + odd]
-                expo = jnp.exp(scores - jnp.max(scores, axis=-1, keepdims=True))
-                scale = 1.0 / jnp.sum(expo, axis=-1, keepdims=True)
-                outs.append(
-                    jnp.dot(
-                        (expo * scale).astype(jnp.bfloat16), contents[part, cols],
-                        preferred_element_type=jnp.float32,
-                    )
-                )
+            return slice(first, first + rows), slice(pair * 2 * HEAD, (pair + 1) * 2 * HEAD)
+
+        scores, expos, totals, outs = {}, {}, {}, {}
+        for unit in units:
+            pair, sample, odd = unit
+            part = parts(pair, sample)
+            chosen = jnp.where(lane // HEAD == odd, query[part], 0)
+            scores[unit] = lax.dot_general(
+                chosen, keys[part], (((1,), (1,)), ((), ())), preferred_element_type=jnp.float32
+            ) + biases[axis, group * 4 + pair * 2 + odd]
+        for unit in units:
+            expos[unit] = jnp.exp(scores[unit] - jnp.max(scores[unit], axis=-1, keepdims=True))
+            totals[unit] = jnp.sum(expos[unit], axis=-1, keepdims=True)
+        for unit in units:
+            outs[unit] = jnp.dot(
+                expos[unit].astype(jnp.bfloat16), contents[parts(*unit[:2])],
+                preferred_element_type=jnp.float32,
+            )
+        for pair, sample, odd in units[::2]:
             place = pl.ds(pl.multiple_of(group * wide + pair * 2 * HEAD, 2 * HEAD), 2 * HEAD)
-            mixed[axis, sample, :, place] = jnp.where(lane < HEAD, outs[0], outs[1]).astype(
-                jnp.bfloat16
-            )
+            even, other = (pair, sample, 0), (pair, sample, 1)
+            mixed[axis, sample, :, place] = jnp.where(
+                lane < HEAD, outs[even] * (1.0 / totals[even]), outs[other] * (1.0 / totals[other])
+            ).astype(jnp.bfloat16)
 
     def returns(group):
         cols = columns_of(group)
@@ -420,40 +443,36 @@
         return copies
 
     def group_step(group, carry):
-        ahead = group + 1
-        more = ahead < groups
+        ahead, later = group + 1, group + 2
         flat = along[...].reshape(3 * samples * rows, features)
         cols = columns_of(group)
 
         def project(which):
             return jnp.dot(flat, full[which, :, cols], preferred_element_type=jnp.float32)
 
-        pl.when(more)(lambda: chain(ahead, 0))
+        def bring(chosen):
+            @pl.when(later < groups)
+            def _():
+                for step in chosen:
+                    from_side(later, step)
+
+        if len(waves) > hops + 1:
+            pl.when(group == 0)(lambda: run(waves[-1:]))
+        pl.when(ahead < groups)(lambda: from_far(ahead))
         query = (project(0) * HEAD ** (-0.5)).astype(jnp.bfloat16)
         keys = project(1).astype(jnp.bfloat16)
         contents = project(2).astype(jnp.bfloat16)
-        pl.when(ahead + 1 < groups)(lambda: own_blocks(ahead + 1))
-        pending = [functools.partial(chain, ahead, step) for step in range(1, levels - 1)]
-        pending += [functools.partial(from_side, ahead, step) for step in range(levels)]
-        pieces = [(axis, pair) for axis in (1, 2, 0) for pair in range(wide // (2 * HEAD))]
-        for number, (axis, pair) in enumerate(pieces):
-            attend(group, axis, pair, query, keys, contents)
-            if number < len(pending):
-                now = [pending[number]] if number + 1 < len(pieces) else pending[number:]
-
-                @pl.when(more)
-                def _():
-                    for act in now:
-                        act()
-
-        for copy in returns(group):
+        bring(range(levels - 2))
+        attend(group, 1, query, keys, contents)
+        bring(range(levels - 2, levels))
+        attend(group, 2, query, keys, contents)
+        copies = returns(group)
+        for copy in copies[: size_y - 1]:
             copy.start()
-
-        @pl.when(more)
-        def _():
-            from_far(ahead)
-            complete(ahead)
-
+        attend(group, 0, query, keys, contents)
+        for copy in copies[size_y - 1 :]:
+            copy.start()
+        pl.when(ahead < groups)(lambda: complete(ahead))
         return carry
 
     lax.fori_loop(0, groups, group_step, 0)

time: 108 us -> 89.1 us (0.82)
  Pallas kernels: 100 us -> 80.9 us
    pallas_call x1, Pallas kernels: 100 us -> 80.9 us  [fast_shards(): pl.pallas_call(functools.partial(fused_kernel, size_y, size_z, rows_z), o...]
where the time goes in v3:
time: 89.1 us; the launch traced here: 88.7 us
  Pallas kernels  80.9 us (91%)
  local copies, waits for them, and re-layouts  5.96 us (7%)
  other arithmetic  1.1 us (1%)
    pallas_call x1, Pallas kernels, fast_shards(): pl.pallas_call(functools.partial(fused_kernel, size_y, size_z, rows_z), o...  80.9 us
    reshape x1, local copies, waits for them, and re-layouts, fast_shards(): return result.reshape(tokens.shape)  2.03 us

profile of v3, /device:TPU:0, one launch (start us, length us, event | category | flops | bytes accessed | tf_op | source)
XLA Modules:
  0.0 88.7 jit_solution(7613389578401793072)
XLA Ops:
  0.0 0.0 copy-start
  0.0 0.0 copy-start.3
  0.0 1.2 %slice_bitcast_fusion.2 = (bf16[1,128,1024]{2,1,0:T(8,128)(2,1)S(1)}, bf16[1,128,1024]{2,1,0:T(8,128)(2,1)S(1)}, bf16[1,128,1024]{2,1,0:T(8,128)(2,1)S(1)}) fusion(bf16[128,3072]{1,0:T(8,128)(2,1)} %param.8), kind=kLoop, calls=%fused_computation.6 | loop fusion | bytes 1572864 | tf_op jit(solution)/shard_map/stack | solution.py:513
  1.2 0.0 copy-done.3
  1.2 0.0 copy-start.1
  1.2 1.1 %pad_maximum_fusion.weights = bf16[4,128,1024]{2,1,0:T(8,128)(2,1)} fusion(bf16[1,128,1024]{2,1,0:T(8,128)(2,1)S(1)} %bitcast.16, bf16[1,128,1024]{2,1,0:T(8,128)(2,1)S(1)} %get-tuple-element.6, bf16[1,128,1024]{2,1,0:T(8,128)(2,1)S(1)} %get-tuple-element.7, bf16[1,128,1024]{2,1,0:T(8,128)(2,1)S(1)} %get-tuple-element.5), kind=kLoop, calls=%fused_computation.3 | loop fusion | flops 1572864 | bytes 2097152 | tf_op jit(solution)/shard_map/stack | solution.py:513
  2.3 0.0 copy-done.1
  2.3 0.0 copy-start.2
  2.3 1.0 %reshape.9.tokens = bf16[2,128,1024]{2,1,0:T(8,128)(2,1)} reshape(bf16[2,64,1,2,1024]{4,3,2,1,0:T(2,128)(2,1)S(1)} %copy-done.1) | data formatting | bytes 1048576 | tf_op jit(solution)/shard_map/reshape | solution.py:537
  3.3 0.0 copy-done
  3.3 0.0 copy-done.2
  3.3 0.0 copy-start.5
  3.3 0.0 copy-start.6
  3.3 0.3 fusion.1
  3.7 0.5 copy-done.5
  4.1 0.0 copy-done.6
  4.1 0.0 copy-start.4
  4.1 0.2 convolution_add_fusion.1
  4.3 0.6 copy-done.4
  4.9 0.0 copy-done.7
  4.9 0.2 fusion
  5.1 0.6 reshape.10.offsets
  5.8 80.9 %shard_map.73 = bf16[2,128,1024]{2,1,0:T(8,128)(2,1)} custom-call(bf16[2,128,1024]{2,1,0:T(8,128)(2,1)} %reshape.9.tokens, bf16[4,128,1024]{2,1,0:T(8,128)(2,1)} %pad_maximum_fusion.weights, f32[4,4,768]{2,1,0:T(4,128)} %reshape.10.offsets), custom_call_target="tpu_custom_call" | custom-call | tf_op jit(solution)/shard_map/pallas_call | solution.py:515
  86.7 2.0 %reshape.11 = bf16[2,64,1,2,1024]{4,3,1,0,2:T(2,128)(2,1)} reshape(bf16[2,128,1024]{2,1,0:T(8,128)(2,1)} %shard_map.73) | data formatting | bytes 1048576 | tf_op jit(solution)/shard_map/reshape | solution.py:538
  (1 shorter events, 0.0 us)
Async XLA Ops:
  0.0 3.3 %copy-start = (f32[16,127]{1,0:T(8,128)S(1)}, f32[16,127]{1,0:T(8,128)}, u32[]{:S(2)}) copy-start(f32[16,127]{1,0:T(8,128)} %param.10) | copy-start | bytes 24388
  0.0 1.2 %copy-start.3 = (bf16[128,1024]{1,0:T(8,128)(2,1)S(1)}, bf16[128,1024]{1,0:T(8,128)(2,1)}, u32[]{:S(2)}) copy-start(bf16[128,1024]{1,0:T(8,128)(2,1)} %param.9) | copy-start | bytes 786436
  1.2 1.1 %copy-start.1 = (bf16[2,64,1,2,1024]{4,3,2,1,0:T(2,128)(2,1)S(1)}, bf16[2,64,1,2,1024]{4,3,2,1,0:T(2,128)(2,1)}, u32[]{:S(2)}) copy-start(bf16[2,64,1,2,1024]{4,3,2,1,0:T(2,128)(2,1)} %param.7) | copy-start | bytes 1572868
  2.3 1.0 %copy-start.2 = (f32[127,768]{1,0:T(8,128)S(1)}, f32[127,768]{1,0:T(8,128)}, u32[]{:S(2)}) copy-start(f32[127,768]{1,0:T(8,128)} %constant.4) | copy-start | bytes 1170436
  3.3 0.8 copy-start.5
  3.3 0.8 copy-start.6
  4.1 0.8 copy-start.4
  4.1 0.8 copy-start.7
